TPU v7x, 32 devices: a whole 2x2x4 slice. The times are simulated.
32 devices in a mesh: pod: 2 (over x), dp: 4 (over z), sp: 4 (over y, core).
Axes of the slice: x: 2, y: 2, z: 4, core: 2. Of those that a mesh axis runs over, the one named last changes fastest.
Arguments:
- x: bfloat16 [8, 128, 256, 1152], P(('pod', 'dp'), 'sp'), parts along dimension 0
- norm_gain: bfloat16 [2, 2, 1152], replicated
- norm_shift: bfloat16 [2, 2, 1152], replicated
- w_qkv: bfloat16 [2, 3, 1152, 16, 72], replicated
- w_out: bfloat16 [2, 16, 72, 1152], replicated
- w_up: bfloat16 [2, 1152, 4608], replicated
- w_down: bfloat16 [2, 4608, 1152], replicated
Outputs:
- output: bfloat16 [8, 128, 256, 1152], P(('pod', 'dp'), 'sp'), parts along dimension 0
There are 2 independent parts. A program takes and returns all parts, laid end to end along the dimension named above; an argument that names none is the same for every part.
All inputs are finite; a program needn't handle non-finite values.
Results may differ from a plain program's by a relative error of at most 0.0155992.
Values are sent between devices in bfloat16 or wider.
A program may use at most 1 GiB of HBM per device.

v0:
```python
import jax
import jax.numpy as jnp
from jax import lax
from jax.sharding import PartitionSpec as P

LN_EPS = 1e-6
SPATIAL_SCORE = 'btshe,btrhe->bthsr'
SPATIAL_MIX = 'bthsr,btrhe->btshe'
TEMPORAL_SCORE = 'btshe,bushe->bshtu'
TEMPORAL_MIX = 'bshtu,bushe->btshe'


def layer_norm(tokens, gain, shift):
    tok_f = tokens.astype(jnp.float32)
    mean_val = jnp.mean(tok_f, axis=-1, keepdims=True)
    centered = tok_f - mean_val
    var_val = jnp.mean(centered * centered, axis=-1, keepdims=True)
    normed = centered * lax.rsqrt(var_val + LN_EPS)
    return (normed * gain.astype(jnp.float32) + shift.astype(jnp.float32)).astype(jnp.bfloat16)


def attn_inputs(tokens, gains, shifts, w_qkv):
    normed = layer_norm(tokens, gains[0], shifts[0])
    return jnp.einsum('btsd,kdhe->kbtshe', normed, w_qkv, preferred_element_type=jnp.float32).astype(jnp.bfloat16)


def attn_core(proj_qkv, score_form, mix_form):
    head_dim = proj_qkv.shape[-1]
    scores = jnp.einsum(score_form, proj_qkv[0], proj_qkv[1], preferred_element_type=jnp.float32) * (head_dim ** -0.5)
    attn_probs = jax.nn.softmax(scores, axis=-1).astype(jnp.bfloat16)
    return jnp.einsum(mix_form, attn_probs, proj_qkv[2], preferred_element_type=jnp.float32).astype(jnp.bfloat16)


def block_tail(tokens, mixed, gains, shifts, w_out, w_up, w_down):
    attn_proj = jnp.einsum('btshe,hed->btsd', mixed, w_out, preferred_element_type=jnp.float32).astype(jnp.bfloat16)
    hidden = (tokens.astype(jnp.float32) + attn_proj.astype(jnp.float32)).astype(jnp.bfloat16)
    normed_mlp = layer_norm(hidden, gains[1], shifts[1])
    up_proj = jnp.dot(normed_mlp, w_up, preferred_element_type=jnp.float32).astype(jnp.bfloat16)
    activated = jax.nn.gelu(up_proj.astype(jnp.float32), approximate=True).astype(jnp.bfloat16)
    down_proj = jnp.dot(activated, w_down, preferred_element_type=jnp.float32).astype(jnp.bfloat16)
    return (hidden.astype(jnp.float32) + down_proj.astype(jnp.float32)).astype(jnp.bfloat16)


def value_a9(tokens, gains, shifts, w_qkv, w_out, w_up, w_down, score_form, mix_form):
    mixed = attn_core(attn_inputs(tokens, gains, shifts, w_qkv), score_form, mix_form)
    return block_tail(tokens, mixed, gains, shifts, w_out, w_up, w_down)


def solution(mesh):
    tok_spec = P(('pod', 'dp'), 'sp', None, None)

    def local_step(x_loc, norm_gain, norm_shift, w_qkv, w_out, w_up, w_down):
        spatial_out = value_a9(x_loc, norm_gain[0], norm_shift[0], w_qkv[0], w_out[0], w_up[0], w_down[0], SPATIAL_SCORE, SPATIAL_MIX)
        by_patch = lax.all_to_all(spatial_out, 'sp', 2, 1, tiled=True)
        temporal_out = value_a9(by_patch, norm_gain[1], norm_shift[1], w_qkv[1], w_out[1], w_up[1], w_down[1], TEMPORAL_SCORE, TEMPORAL_MIX)
        return lax.all_to_all(temporal_out, 'sp', 1, 2, tiled=True)

    return jax.shard_map(local_step, mesh=mesh, in_specs=(tok_spec, P(), P(), P(), P(), P(), P()), out_specs=tok_spec, check_vma=False)
```

profile of v0, /device:TPU:0, one launch (start us, length us, event | category | flops | bytes accessed | tf_op | source)
XLA Modules:
  0.0 1584.0 jit_solution(3519762678375446363)
XLA Ops:
  0.0 0.0 copy-start
  0.0 0.0 copy-start.1
  0.0 11.3 convert_reduce_fusion.2
  11.3 8.5 fusion.40
  19.9 0.0 copy-done
  19.9 0.0 copy-done.1
  19.9 0.7 convert_reduce_fusion.3
  20.6 86.1 %convert_bitcast_fusion.1 = bf16[3,1,32,256,16,72]{3,5,4,0,2,1:T(8,128)(2,1)} fusion(bf16[1,32,256,1152]{3,2,1,0:T(8,128)(2,1)} %param.7, f32[1152]{0:T(1024)S(1)} %get-tuple-element.11, f32[1152]{0:T(1024)S(1)} %get-tuple-element.22, f32[32,256]{1,0:T(8,128)S(1)} %add_rsqrt_fusion.3, f32[32,256]{1,0:T(8,128)S(1)} %broadcast_multiply_fusion.3, ...), kind=kOutput, calls=%fused_computation.35 | convolution fusion | flops 65314750464 | bytes 83534848 | tf_op jit(solution)/shard_map/btsd,kdhe->kbtshe/dot_general | solution.py:24
  106.7 59.6 %fusion.64 = f32[32,16,256,256]{2,3,1,0:T(8,128)} fusion(bf16[3,1,32,256,16,72]{3,5,4,0,2,1:T(8,128)(2,1)} %convert_bitcast_fusion.1), kind=kOutput, calls=%fused_computation.87 | convolution fusion | flops 4831838208 | bytes 171966464 | tf_op jit(solution)/shard_map/btshe,btrhe->bthsr/dot_general | solution.py:29
  166.3 128.4 %fusion.119 = (f32[32,16,256]{2,1,0:T(8,128)S(1)}, f32[32,16,256,256]{2,3,1,0:T(8,128)}) fusion(f32[32,16,256,256]{2,3,1,0:T(8,128)} %fusion.64), kind=kOutput, calls=%fused_computation.148 | output fusion | flops 134217984 | bytes 268959744 | tf_op jit(solution)/shard_map/sub | solution.py:30
  294.7 0.0 copy-start.6
  294.7 0.0 copy-start.7
  294.7 65.3 %convert_reduce_fusion.1 = (f32[32,256]{1,0:T(8,128)S(1)}, bf16[1,32,256,1152]{3,2,1,0:T(8,128)(2,1)}) fusion(bf16[2,16,72,1152]{3,2,1,0:T(8,128)(2,1)} %param.11, f32[32,16,256,256]{2,3,1,0:T(8,128)} %get-tuple-element.14, f32[32,16,256]{2,1,0:T(8,128)S(1)} %get-tuple-element.13, bf16[3,1,32,256,16,72]{3,5,4,0,2,1:T(8,128)(2,1)} %convert_bitcast_fusion.1, ...), kind=kOutput, calls=%fused_computation.41 | convolution fusion | flops 26717708288 | bytes 194052096 | tf_op jit(solution)/shard_map/btshe,hed->btsd/dot_general | solution.py:35
  360.0 8.5 fusion.36
  368.5 0.0 copy-done.6
  368.5 0.0 copy-done.7
  368.5 109.6 %fusion.59 = bf16[32,256,4608]{2,1,0:T(8,128)(2,1)} fusion(bf16[1,32,256,1152]{3,2,1,0:T(8,128)(2,1)} %get-tuple-element.16, f32[1152]{0:T(1024)S(1)} %copy-done.6, f32[1152]{0:T(1024)S(1)} %copy-done.7, f32[32,256]{1,0:T(8,128)S(1)} %add_rsqrt_fusion.2, f32[32,256]{1,0:T(8,128)S(1)} %broadcast_multiply_fusion.2, bf16[2,1152,4608]{2,1,0:T(8,128)(2,1)} %param.12), kind=kOutput, calls=%fused_computation.80 | convolution fusion | flops 87029710848 | bytes 105063424 | tf_op jit(solution)/shard_map/dot_general | solution.py:38
  478.1 121.5 %fusion.45 = bf16[1,32,256,1152]{3,2,1,0:T(8,128)(2,1)} fusion(bf16[1,32,256,1152]{3,2,1,0:T(8,128)(2,1)} %get-tuple-element.16, bf16[32,256,4608]{2,1,0:T(8,128)(2,1)} %fusion.59, bf16[2,4608,1152]{2,1,0:T(8,128)(2,1)} %param.13), kind=kOutput, calls=%fused_computation.64 | convolution fusion | flops 87397761024 | bytes 123863040 | tf_op jit(solution)/shard_map/dot_general | solution.py:40
  599.6 16.3 %copy.14 = bf16[1,32,256,1152]{3,1,0,2:T(8,128)(2,1)S(1)} copy(bf16[1,32,256,1152]{3,2,1,0:T(8,128)(2,1)} %fusion.45) | data formatting | bytes 37748736 | tf_op jit(solution)/shard_map/convert_element_type | solution.py:41
  615.9 209.5 %all_to_all.27 = bf16[1,32,256,1152]{3,1,0,2:T(8,128)(2,1)S(1)} all-to-all(bf16[1,32,256,1152]{3,1,0,2:T(8,128)(2,1)S(1)} %copy.14), channel_id=1, replica_groups=mesh['pod'=2,'dp'=4,'sp'=4] {'sp'}, dimensions={2} | all-to-all | bytes 37748736 | tf_op jit(solution)/shard_map/all_to_all | solution.py:54
  825.5 10.7 bitcast_reduce_fusion
  836.1 0.0 copy-start.2
  836.2 0.0 copy-start.3
  836.2 12.9 copy.15
  849.1 0.0 slice-start
  849.1 0.0 slice-start.1
  849.1 6.2 multiply_reduce_fusion.2
  855.4 0.1 add_rsqrt_fusion
  855.4 0.0 copy-done.2
  855.4 0.0 copy-done.3
  855.4 0.0 slice-start.2
  855.5 0.0 slice-start.3
  855.5 11.0 add_convert_fusion.1
  866.5 0.0 slice-done
  866.5 0.0 slice-done.1
  866.5 0.0 slice-done.2
  866.5 0.0 slice-done.3
  866.5 81.2 %convert_bitcast_fusion = bf16[3,1,128,64,16,72]{2,5,4,0,3,1:T(8,128)(2,1)} fusion(bf16[128,64,1152,1,1]{2,0,4,3,1:T(8,128)(2,1)} %bitcast.213, bf16[2,3,1152,16,72]{2,4,3,1,0:T(8,128)(2,1)S(1)} %bitcast.215), kind=kOutput, calls=%fused_computation.34 | convolution fusion | flops 65258127360 | bytes 83460096 | tf_op jit(solution)/shard_map/btsd,kdhe->kbtshe/dot_general | solution.py:24
  947.8 34.8 %fusion.63 = f32[64,16,128,128]{2,3,1,0:T(8,128)} fusion(bf16[3,1,128,64,16,72]{2,5,4,0,3,1:T(8,128)(2,1)} %convert_bitcast_fusion), kind=kOutput, calls=%fused_computation.83 | convolution fusion | flops 2415919104 | bytes 104857600 | tf_op jit(solution)/shard_map/btshe,bushe->bshtu/dot_general | solution.py:29
  982.6 68.4 %fusion.120 = (f32[64,16,128]{2,1,0:T(8,128)S(1)}, f32[64,16,128,128]{2,3,1,0:T(8,128)}) fusion(f32[64,16,128,128]{2,3,1,0:T(8,128)} %fusion.63), kind=kOutput, calls=%fused_computation.149 | output fusion | flops 67108992 | bytes 134742016 | tf_op jit(solution)/shard_map/sub | solution.py:30
  1050.9 0.0 copy-start.4
  1050.9 0.0 copy-start.5
  1051.0 53.1 %convert_reduce_fusion = (f32[128,64]{0,1:T(8,128)S(1)}, bf16[128,64,1152]{2,0,1:T(8,128)(2,1)}) fusion(f32[128,64,1152]{2,0,1:T(8,128)} %bitcast.212, bf16[2,16,72,1152]{3,2,1,0:T(8,128)(2,1)} %param.11, f32[64,16,128,128]{2,3,1,0:T(8,128)} %get-tuple-element.18, f32[64,16,128]{2,1,0:T(8,128)S(1)} %get-tuple-element.17, ...), kind=kOutput, calls=%fused_computation.38 | convolution fusion | flops 24258797568 | bytes 145817600 | tf_op jit(solution)/shard_map/btshe,hed->btsd/dot_general | solution.py:35
  1104.1 8.5 fusion.32
  1112.6 0.0 copy-done.4
  1112.6 0.0 copy-done.5
  1112.6 131.4 %fusion.160 = bf16[128,64,4608]{2,0,1:T(8,128)(2,1)} fusion(bf16[128,64,1152]{2,0,1:T(8,128)(2,1)} %get-tuple-element.20, f32[1152]{0:T(1024)S(1)} %copy-done.4, f32[1152]{0:T(1024)S(1)} %copy-done.5, f32[128,64]{0,1:T(8,128)S(1)} %add_rsqrt_fusion.1, f32[128,64]{0,1:T(8,128)S(1)} %broadcast_multiply_fusion.1, ...), kind=kOutput, calls=%fused_computation.21.clone.clone.clone.clone.clone.clone.2 | convolution fusion | flops 87444946944 | bytes 105063424 | tf_op jit(solution)/shard_map/dot_general | solution.py:38
  1244.1 107.8 %fusion.55 = bf16[1,128,64,1152]{3,1,2,0:T(8,128)(2,1)} fusion(bf16[128,64,1152]{2,0,1:T(8,128)(2,1)} %get-tuple-element.20, bf16[2,4608,1152]{2,1,0:T(8,128)(2,1)} %param.13, bf16[128,64,4608]{2,0,1:T(8,128)(2,1)} %fusion.160), kind=kOutput, calls=%fused_computation.77 | convolution fusion | flops 87020273664 | bytes 123863040 | tf_op jit(solution)/shard_map/dot_general | solution.py:40
  1351.9 16.3 %copy.17 = bf16[1,128,64,1152]{3,2,0,1:T(8,128)(2,1)S(1)} copy(bf16[1,128,64,1152]{3,1,2,0:T(8,128)(2,1)} %fusion.55) | data formatting | bytes 37748736 | tf_op jit(solution)/shard_map/convert_element_type | solution.py:41
  1368.2 208.6 %all_to_all.28 = bf16[1,128,64,1152]{3,2,0,1:T(8,128)(2,1)S(1)} all-to-all(bf16[1,128,64,1152]{3,2,0,1:T(8,128)(2,1)S(1)} %copy.17), channel_id=1, replica_groups=mesh['pod'=2,'dp'=4,'sp'=4] {'sp'}, dimensions={1} | all-to-all | bytes 37748736 | tf_op jit(solution)/shard_map/all_to_all | solution.py:56
  1576.9 6.9 copy.18
  (8 shorter events, 0.1 us)
Async XLA Ops:
  0.0 19.9 %copy-start = (bf16[2,2,1152]{2,1,0:T(2,128)(2,1)S(1)}, bf16[2,2,1152]{2,1,0:T(2,128)(2,1)}, u32[]{:S(2)}) copy-start(bf16[2,2,1152]{2,1,0:T(2,128)(2,1)} %param.9) | copy-start | bytes 27652
  0.0 19.9 %copy-start.1 = (bf16[2,2,1152]{2,1,0:T(2,128)(2,1)S(1)}, bf16[2,2,1152]{2,1,0:T(2,128)(2,1)}, u32[]{:S(2)}) copy-start(bf16[2,2,1152]{2,1,0:T(2,128)(2,1)} %param.8) | copy-start | bytes 27652
  294.7 73.8 %copy-start.6 = (f32[1152]{0:T(1024)S(1)}, f32[1152]{0:T(1024)}, u32[]{:S(2)}) copy-start(f32[1152]{0:T(1024)} %get-tuple-element.10) | copy-start | bytes 13828
  294.7 73.8 %copy-start.7 = (f32[1152]{0:T(1024)S(1)}, f32[1152]{0:T(1024)}, u32[]{:S(2)}) copy-start(f32[1152]{0:T(1024)} %get-tuple-element.23) | copy-start | bytes 13828
  836.1 19.3 %copy-start.2 = (f32[1152]{0:T(1024)S(1)}, f32[1152]{0:T(1024)}, u32[]{:S(2)}) copy-start(f32[1152]{0:T(1024)} %get-tuple-element.12) | copy-start | bytes 13828
  836.2 19.3 %copy-start.3 = (f32[1152]{0:T(1024)S(1)}, f32[1152]{0:T(1024)}, u32[]{:S(2)}) copy-start(f32[1152]{0:T(1024)} %get-tuple-element.21) | copy-start | bytes 13828
  849.1 17.4 %slice-start = ((s8[15925248]{0:T(1024)(128)(4,1)}), s8[4194304]{0:T(1024)(128)(4,1)S(1)}, s32[]{:S(2)}) async-start(s8[15925248]{0:T(1024)(128)(4,1)} %bitcast.214), calls=%async_computation.2 | async-start | bytes 8388608
  849.1 17.4 %slice-start.1 = ((s8[15925248]{0:T(1024)(128)(4,1)}), s8[4194304]{0:T(1024)(128)(4,1)S(1)}, s32[]{:S(2)}) async-start(s8[15925248]{0:T(1024)(128)(4,1)} %bitcast.214), calls=%async_computation.3 | async-start | bytes 8388608
  855.4 11.0 slice-start.2
  855.5 11.0 slice-start.3
  1050.9 61.6 %copy-start.4 = (f32[1152]{0:T(1024)S(1)}, f32[1152]{0:T(1024)}, u32[]{:S(2)}) copy-start(f32[1152]{0:T(1024)} %get-tuple-element.9) | copy-start | bytes 13828
  1050.9 61.6 %copy-start.5 = (f32[1152]{0:T(1024)S(1)}, f32[1152]{0:T(1024)}, u32[]{:S(2)}) copy-start(f32[1152]{0:T(1024)} %get-tuple-element.24) | copy-start | bytes 13828
where the time goes:
time: 1590 us; the launch traced here: 1580 us
  matrix products  850 us (53%)
  blocking collectives  418 us (26%)
  other arithmetic  262 us (16%)
  local copies, waits for them, and re-layouts  52.6 us (3%)
    dot_general x2, matrix products, block_tail(): jnp.dot(normed_mlp, w_up, preferred_element_type=jnp.float32)  241 us
    dot_general x2, matrix products, block_tail(): jnp.dot(activated, w_down, preferred_element_type=jnp.float32)  229 us
    all_to_all x1, blocking collectives, local_step(): by_patch = lax.all_to_all(spatial_out, 'sp', 2, 1, tiled=True)  210 us
    all_to_all x1, blocking collectives, local_step(): return lax.all_to_all(temporal_out, 'sp', 1, 2, tiled=True)  209 us
    sub x2, other arithmetic, attn_core(): attn_probs = jax.nn.softmax(scores, axis=-1).astype(jnp.bfloat16)  197 us
    dot_general x2, matrix products, attn_inputs(): jnp.einsum('btsd,kdhe->kbtshe', normed, w_qkv, preferred_element_type=jnp...  167 us
    dot_general x2, matrix products, block_tail(): jnp.einsum('btshe,hed->btsd', mixed, w_out, preferred_element_type=jnp.fl...  118 us
    dot_general x2, matrix products, attn_core(): jnp.einsum(score_form, proj_qkv[0], proj_qkv[1], preferred_element_type=j...  94.4 us

commit v1 on v0

v1 whole, which is shorter than its diff:
```python
import functools
import math

import jax
import jax.numpy as jnp
from jax import lax
from jax.experimental import pallas as pl
from jax.experimental.pallas import tpu as pltpu
from jax.sharding import PartitionSpec as P

F32, BF = jnp.float32, jnp.bfloat16
D, H, E, FF = 1152, 16, 72, 4608
EP = 80
LN_EPS = 1e-6
NN = (((1,), (0,)), ((), ()))
NT = (((1,), (1,)), ((), ()))
TN = (((0,), (0,)), ((), ()))
CEXP = E ** -0.5 * math.log2(math.e)
SLOTS = 4
QC = 576
UC = 256
DC = 256
LANES = 128
G = 8
MESH = pl.DeviceIdType.MESH


def dg(a, b, dims):
    return lax.dot_general(a, b, dims, preferred_element_type=F32)


def ln(tok, gain, shift):
    mean = jnp.sum(tok, axis=-1, keepdims=True) * (1.0 / D)
    cen = tok - mean
    var = jnp.sum(cen * cen, axis=-1, keepdims=True) * (1.0 / D)
    return cen * lax.rsqrt(var + LN_EPS) * gain + shift


def gelu(u):
    u = u.astype(BF).astype(F32)
    t = jnp.tanh(u * (0.7978845608028654 + 0.035677408136300125 * (u * u)))
    half = 0.5 * u
    return (half + half * t).astype(BF)


def interleave(main, side, weights):
    total, done, k = sum(weights), 0.0, 0
    for thunk, w in zip(main, weights):
        goal = int(done / total * len(side)) + 1
        while k < min(goal, len(side)):
            side[k]()
            k += 1
        thunk()
        done += w
    for thunk in side[k:]:
        thunk()


def peer_of(k):
    me = lax.axis_index("sp")
    yy, cc = me // 2, me % 2
    return 2 * ((yy + k // 2) % 2) + (cc + k % 2) % 2


def entry_barrier():
    bar = pltpu.get_barrier_semaphore()
    for k in (1, 2, 3):
        pl.semaphore_signal(bar, inc=1, device_id={"sp": peer_of(k)}, device_id_type=MESH)
    pl.semaphore_wait(bar, 3)


def col_max(s_ref, k, rows, step=32):
    m = None
    for r in range(0, rows, step):
        t = jnp.max(s_ref[k, r:r + step, :].reshape(step // 8, 8, -1), axis=0)
        m = t if m is None else jnp.maximum(m, t)
    return jnp.max(m, axis=0, keepdims=True)


def softmax_cols(s_ref, k, rows, put, step=32):
    mc = col_max(s_ref, k, rows) * CEXP
    d = None
    for r in range(0, rows, step):
        e = jnp.exp2(s_ref[k, r:r + step, :] * CEXP - mc)
        s_ref[k, r:r + step, :] = e
        t = jnp.sum(e.reshape(step // 8, 8, -1), axis=0)
        d = t if d is None else d + t
    inv = 1.0 / jnp.sum(d, axis=0, keepdims=True)
    for r in range(0, rows, step):
        put(r, step, s_ref[k, r:r + step, :] * inv)


def head_sides(scores, soft, mix, oT_ref):
    pend = {}

    def side(h):
        if h < H:
            scores(h)
        if 0 <= h - 1 < H:
            soft(h - 1)
        if 0 <= h - 2 < H:
            pend[h - 2] = mix(h - 2)[:E]
            if h % 2:
                j = (h - 2) // 2
                pair = jnp.concatenate([pend.pop(2 * j), pend.pop(2 * j + 1)], axis=0)
                oT_ref[2 * E * j:2 * E * (j + 1), :] = pair.astype(BF)

    return [functools.partial(side, h) for h in range(H + 2)]


def load_weights(pairs, sem):
    return [pltpu.make_async_copy(src, dst, sem.at[i]) for i, (src, dst) in enumerate(pairs)]


def spatial_kernel(FR, NPQ, x_ref, xn_ref, gain_ref, shift_ref, wq_hbm, wo_hbm, wu_hbm, wd_hbm, xs_hbm, rcv_hbm,
                   wq, wo, wu, wd, n1, hh, qkv, s_ref, p_ref, oT, n2, g_ref, obuf, wsem, lsem, ssem, rsem):
    i = pl.program_id(0)
    NP = 4 * NPQ
    me = lax.axis_index("sp")
    loads = load_weights([(wq_hbm.at[0], wq), (wo_hbm.at[0], wo), (wu_hbm.at[0], wu), (wd_hbm.at[0], wd)], wsem)
    g1, b1 = gain_ref[0, 0:1, :].astype(F32), shift_ref[0, 0:1, :].astype(F32)
    g2, b2 = gain_ref[0, 1:2, :].astype(F32), shift_ref[0, 1:2, :].astype(F32)

    def copies(slot, f):
        local = [
            pltpu.make_async_copy(obuf.at[slot], xs_hbm.at[:, f], lsem.at[slot, 0]),
            pltpu.make_async_copy(obuf.at[slot, me], rcv_hbm.at[me, f], lsem.at[slot, 1]),
        ]
        remote = [
            pltpu.make_async_remote_copy(
                src_ref=obuf.at[slot, peer_of(k)], dst_ref=rcv_hbm.at[me, f],
                send_sem=ssem.at[slot, k - 1], recv_sem=rsem.at[k - 1],
                device_id={"sp": peer_of(k)}, device_id_type=MESH)
            for k in (2, 3, 1)
        ]
        return local, remote

    def wait_slot(slot, f):
        local, remote = copies(slot, f)
        for c in local:
            c.wait()
        for c in remote:
            c.wait_send()

    def step(do_a, do_b):
        f = i - 1
        slot = lax.rem(f + 2, 2)
        if do_b:
            pl.when(f >= 2)(lambda: wait_slot(slot, f - 2))

        def ln1(src):
            def part(r):
                n1[r:r + 64, :] = ln(src[0, r:r + 64, :].astype(F32), g1, b1).astype(BF)
            return [functools.partial(part, r) for r in range(0, NP, 64)]

        def ln2_part(r):
            n2[r:r + 64, :] = ln(hh[r:r + 64, :].astype(F32), g2, b2).astype(BF)

        def proj(t, c):
            r = dg(wq[t * D + c * QC:t * D + (c + 1) * QC, :], n1[...], NT)
            z = jnp.zeros((EP - E, NP), F32)
            for h in range(QC // E):
                qkv[t, c * (QC // E) + h] = jnp.concatenate([r[h * E:(h + 1) * E], z], axis=0).astype(BF)

        def up(c):
            u = dg(n2[...], wu[:, c * UC:(c + 1) * UC], NN)
            g_ref[:, c * UC:(c + 1) * UC] = gelu(u)

        def down(c):
            e = min(c + DC, D)
            m = dg(g_ref[...], wd[:, c:e], NN).astype(BF).astype(F32)
            for q in range(4):
                old = obuf[slot, q, :, c:e].astype(F32)
                obuf[slot, q, :, c:e] = (old + m[q * NPQ:(q + 1) * NPQ]).astype(BF)

        def outp():
            a = dg(oT[...], wo[...], TN).astype(BF)
            hh[...] = (x_ref[0].astype(F32) + a.astype(F32)).astype(BF)

        def scores(h):
            s_ref[h % SLOTS] = dg(qkv[1, h], qkv[0, h], TN)

        def soft(h):
            k = h % SLOTS

            def put(r, n, v):
                p_ref[k, r:r + n, :] = v.astype(BF)
            softmax_cols(s_ref, k, NP, put)

        def mix(h):
            return dg(qkv[2, h], p_ref[h % SLOTS], NN)

        projs = [functools.partial(proj, t, c) for c in range(D // QC) for t in range(3)]
        ups = [functools.partial(up, c) for c in range(FF // UC)]
        downs = [functools.partial(down, c) for c in range(0, D, DC)]
        heads = head_sides(scores, soft, mix, oT)
        ln2s = [functools.partial(ln2_part, r) for r in range(0, NP, 64)]

        if do_b:
            for q in range(4):
                obuf[slot, q] = hh[q * NPQ:(q + 1) * NPQ, :]
        if do_a and do_b:
            interleave(projs, ln2s, [1.0] * len(projs))
            interleave(ups + downs[:-1], heads, [5.0] * len(ups) + [18.0] * (len(downs) - 1))
            interleave([outp, downs[-1]], ln1(xn_ref), [0.0, 1.0])
        elif do_a:
            for th in ln1(x_ref) + projs + heads + [outp] + ln1(xn_ref):
                th()
        else:
            for th in ln2s + ups + downs:
                th()

        if do_b:
            local, remote = copies(slot, f)
            for c in remote + local:
                c.start()

    @pl.when(i == 0)
    def _():
        for c in loads:
            c.start()
        entry_barrier()
        for c in loads[:2]:
            c.wait()
        step(True, False)

    @pl.when(i == 1)
    def _():
        for c in loads[2:]:
            c.wait()

    pl.when((i > 0) & (i < FR))(lambda: step(True, True))

    @pl.when(i == FR)
    def _():
        step(False, True)
        for f in (FR - 2, FR - 1):
            wait_slot(f % 2, f)
        for k in (1, 2, 3):
            src = peer_of(k)
            pltpu.make_async_copy(rcv_hbm.at[src], rcv_hbm.at[src], rsem.at[k - 1]).wait()


def spatial(x, gain, shift, wq, wo, wu, wd):
    FR, NP, _ = x.shape
    NPQ = NP // 4
    any_spec = pl.BlockSpec(memory_space=pl.ANY)
    vm = pltpu.VMEM
    part = jax.ShapeDtypeStruct((4, FR, NPQ, D), BF)
    flops = 2 * FR * NP * (4 * D * D + 2 * D * FF) + 4 * FR * NP * NP * D
    return pl.pallas_call(
        functools.partial(spatial_kernel, FR, NPQ),
        grid=(FR + 1,),
        in_specs=[
            pl.BlockSpec((1, NP, D), lambda i: (jnp.minimum(i, FR - 1), 0, 0)),
            pl.BlockSpec((1, NP, D), lambda i: (jnp.minimum(i + 1, FR - 1), 0, 0)),
            pl.BlockSpec((2, 2, D), lambda i: (0, 0, 0)),
            pl.BlockSpec((2, 2, D), lambda i: (0, 0, 0)),
            any_spec, any_spec, any_spec, any_spec,
        ],
        out_specs=[any_spec, any_spec],
        out_shape=[part, part],
        scratch_shapes=[
            vm((3 * D, D), BF), vm((D, D), BF), vm((D, FF), BF), vm((FF, D), BF),
            vm((NP, D), BF), vm((NP, D), BF), vm((3, H, EP, NP), BF),
            vm((SLOTS, NP, NP), F32), vm((SLOTS, NP, NP), BF), vm((D, NP), BF),
            vm((NP, D), BF), vm((NP, FF), BF), vm((2, 4, NPQ, D), BF),
            pltpu.SemaphoreType.DMA((4,)), pltpu.SemaphoreType.DMA((2, 2)),
            pltpu.SemaphoreType.DMA((2, 3)), pltpu.SemaphoreType.DMA((3,)),
        ],
        compiler_params=pltpu.CompilerParams(
            collective_id=0, has_side_effects=True, vmem_limit_bytes=60 * 1024 * 1024,
            dimension_semantics=("arbitrary",)),
        cost_estimate=pl.CostEstimate(flops=flops, bytes_accessed=4 * x.size * 2, transcendentals=0),
        name="spatial",
    )(x, x, gain, shift, wq, wo, wu, wd)


def temporal_kernel(FR, NPQ, rcv_hbm, xs_hbm, gain_ref, shift_ref, wq_hbm, wo_hbm, wu_hbm, wd_hbm,
                    y_hbm, o_hbm, orcv_hbm,
                    wq, wo, wu, wsem, xsem, lsem, ssem, rsem, bsem, ysem):
    KF = 4 * FR
    NG = NPQ // G
    T = 2 * KF
    B = FR * G
    NCOL = D // LANES
    S = KF + 8
    PJ = G // 2
    assert PJ == 4
    NT_ = NG * PJ
    me = lax.axis_index("sp")
    loads = load_weights([(wq_hbm.at[1], wq), (wo_hbm.at[1], wo), (wu_hbm.at[1], wu)], wsem)
    for c in loads:
        c.start()
    g1, b1 = gain_ref[1, 0:1, :].astype(F32), shift_ref[1, 0:1, :].astype(F32)
    g2, b2 = gain_ref[1, 1:2, :].astype(F32), shift_ref[1, 1:2, :].astype(F32)
    entry_barrier()

    def send(g, k):
        at = pl.ds(pl.multiple_of(g * G, G), G)
        return pltpu.make_async_remote_copy(
            src_ref=o_hbm.at[peer_of(k), :, at], dst_ref=orcv_hbm.at[me, :, at],
            send_sem=ssem.at[k - 1, g], recv_sem=rsem.at[k - 1, g],
            device_id={"sp": peer_of(k)}, device_id_type=MESH)

    def phase1(nscr, oscr, xblk, nb, qb, kb, vb, s_ref, p_ref, oT, oblk):
        def x_load(g, slot):
            at = pl.ds(pl.multiple_of(g * G, G), G)
            return pltpu.make_async_copy(rcv_hbm.at[:, :, at], xblk.at[slot], xsem.at[slot])

        def o_store(g):
            at = pl.ds(pl.multiple_of(g * G, G), G)
            return [
                pltpu.make_async_copy(oblk, o_hbm.at[:, :, at], lsem.at[0]),
                pltpu.make_async_copy(oblk.at[me], orcv_hbm.at[me, :, at], lsem.at[1]),
            ]

        def ln_part(slot, par, a, r):
            tok = xblk[slot, a, 8 * r:8 * r + 8].astype(F32).reshape(8 * G, D)
            n = ln(tok, g1, b1)
            for fi in range(8):
                f = a * FR + 8 * r + fi
                for c in range(NCOL):
                    nscr[par, c, pl.ds(f, G, stride=S), :] = n[fi * G:(fi + 1) * G, c * LANES:(c + 1) * LANES]

        def take_pair(par, j):
            for e in range(2):
                at = pl.ds(pl.multiple_of((2 * j + e) * S, 8), KF)
                for c in range(NCOL):
                    nb[e * KF:(e + 1) * KF, c * LANES:(c + 1) * LANES] = nscr[par, c, at, :].astype(BF)

        def proj(par, t, c):
            r = dg(wq[t * D + c * QC:t * D + (c + 1) * QC, :], nb[...], NT)
            z = jnp.zeros((EP - E, T), F32)
            for hi in range(QC // E):
                h = c * (QC // E) + hi
                v = jnp.concatenate([r[hi * E:(hi + 1) * E], z], axis=0).astype(BF)
                if t == 2:
                    vb[par, h] = v
                else:
                    for e in range(2):
                        w = v[:, e * KF:(e + 1) * KF]
                        if t == 0:
                            qb[par, h, e * EP:(e + 1) * EP, e * KF:(e + 1) * KF] = w
                        else:
                            kb[par, h, e * EP:(e + 1) * EP, :] = w

        def heads(par):
            def scores(h):
                s_ref[h % SLOTS] = dg(kb[par, h], qb[par, h], TN)

            def soft(h):
                k = h % SLOTS

                def put(r, n, v):
                    v = v.astype(BF)
                    p_ref[k, r:r + n, 0:KF] = v[:, 0:KF]
                    p_ref[k, KF + r:KF + r + n, KF:T] = v[:, KF:T]
                softmax_cols(s_ref, k, KF, put)

            def mix(h):
                return dg(vb[par, h], p_ref[h % SLOTS], NN)

            return head_sides(scores, soft, mix, oT)

        def put_pair(par, j):
            for e in range(2):
                at = pl.ds(pl.multiple_of((2 * j + e) * S, 8), KF)
                for c in range(NCOL):
                    v = oT[c * LANES:(c + 1) * LANES, e * KF:(e + 1) * KF]
                    oscr[par, c, at, :] = jnp.transpose(v).astype(F32)

        def gather_part(par, a, r):
            for fi in range(8):
                f = a * FR + 8 * r + fi
                row = [oscr[par, c, pl.ds(f, G, stride=S), :] for c in range(NCOL)]
                oblk[a, 8 * r + fi] = jnp.concatenate(row, axis=1).astype(BF)

        x_load(0, 0).start()
        x_load(1, 1).start()
        qb[...] = jnp.zeros_like(qb)
        p_ref[...] = jnp.zeros_like(p_ref)
        kb[...] = jnp.zeros_like(kb)
        vb[...] = jnp.zeros_like(vb)
        x_load(0, 0).wait()

        def first(a, _):
            for r in range(FR // 8):
                ln_part(0, 0, a, r)
            return 0
        lax.fori_loop(0, 4, first, 0)
        loads[0].wait()

        def body(t, _):
            g, j = t // PJ, t % PJ
            ga, a = (t + 3) // PJ - 2, (t + 3) % PJ

            @pl.when(j == 0)
            def _():
                @pl.when(g + 1 < NG)
                def _():
                    x_load(g + 1, (g + 1) % 2).wait()

                @pl.when(g + 2 < NG)
                def _():
                    x_load(g + 2, g % 2).start()

            @pl.when((a == 0) & (ga >= 1))
            def _():
                for c in o_store(ga - 1):
                    c.wait()
                for k in (2, 3, 1):
                    send(ga - 1, k).start()

            par, gp = t % 2, g % 2
            hp, hg, hj = (t + 1) % 2, ((t + 7) // PJ) % 2, (t + 7) % PJ
            take_pair(gp, j)
            main = [functools.partial(proj, par, tt, c) for c in range(D // QC) for tt in range(3)]
            side = heads(hp)
            lns = [functools.partial(ln_part, (g + 1) % 2, (g + 1) % 2, j, r) for r in range(FR // 8)]
            gas = [functools.partial(gather_part, (ga + 2) % 2, a, r) for r in range(FR // 8)]
            extra = [th for pair in zip(lns, gas) for th in pair]
            merged, k = [], 0
            for n, th in enumerate(side):
                merged.append(th)
                if n % 2 == 1 and k < len(extra):
                    merged.append(extra[k])
                    k += 1
            merged += extra[k:]
            interleave(main, merged, [1.0] * len(main))
            put_pair(hg, hj)

            @pl.when((a == PJ - 1) & (ga >= 0))
            def _():
                for c in o_store(ga):
                    c.start()
            return 0
        lax.fori_loop(0, NT_, body, 0)

        for th in heads((NT_ - 1) % 2):
            th()
        put_pair((NG - 1) % 2, PJ - 1)

        def finish(g):
            for c in o_store(g):
                c.start()
            for c in o_store(g):
                c.wait()
            for k in (2, 3, 1):
                send(g, k).start()
        for r in range(FR // 8):
            gather_part((NG - 2) % 2, 3, r)
        finish(NG - 2)

        def last(a, _):
            for r in range(FR // 8):
                gather_part((NG - 1) % 2, a, r)
            return 0
        lax.fori_loop(0, 4, last, 0)
        finish(NG - 1)

    NB = 4 * NG

    def phase2(wd, ob, xb, yb, of, hh, n2, g_ref):
        wd_load = pltpu.make_async_copy(wd_hbm.at[1], wd, wsem.at[3])
        wd_load.start()

        def block(b):
            return peer_of(b // NG), b % NG

        def fetch(b, slot):
            owner, g = block(b)
            at = pl.ds(pl.multiple_of(g * G, G), G)
            return [
                pltpu.make_async_copy(orcv_hbm.at[owner, :, at], ob.at[slot], bsem.at[slot, 0]),
                pltpu.make_async_copy(xs_hbm.at[owner, :, at], xb.at[slot], bsem.at[slot, 1]),
            ]

        def arrive(b):
            owner, g = block(b)
            at = pl.ds(pl.multiple_of(g * G, G), G)
            here = orcv_hbm.at[owner, :, at]
            return pltpu.make_async_copy(here, here, rsem.at[b // NG - 1, g])

        def y_store(b, slot):
            owner, g = block(b)
            at = pl.ds(pl.multiple_of(owner * NPQ + g * G, G), G)
            return pltpu.make_async_copy(yb.at[slot], y_hbm.at[:, at], ysem.at[slot])

        def ln2_part(r):
            n2[r:r + 64, :] = ln(hh[r:r + 64, :].astype(F32), g2, b2).astype(BF)
        ln2s = [functools.partial(ln2_part, r) for r in range(0, B, 64)]

        def take(slot, c):
            e = min(c + DC, D)
            of[:, c:e] = ob[slot, :, :, c:e].astype(F32).reshape(B, e - c).astype(BF)

        def outp(slot, c):
            e = min(c + DC, D)
            x = xb[slot, :, :, c:e].astype(F32).reshape(B, e - c)
            a = dg(of[...], wo[:, c:e], NN).astype(BF)
            hh[:, c:e] = (x + a.astype(F32)).astype(BF)

        def up(c):
            u = dg(n2[...], wu[:, c * UC:(c + 1) * UC], NN)
            g_ref[:, c * UC:(c + 1) * UC] = gelu(u)

        def down(slot, c):
            e = min(c + DC, D)
            m = dg(g_ref[...], wd[:, c:e], NN).astype(BF).astype(F32)
            old = yb[slot, :, :, c:e].astype(F32)
            yb[slot, :, :, c:e] = (old + m.reshape(FR, G, e - c)).astype(BF)

        def step(b, do_a, do_b):
            slot, old = b % 2, (b + 1) % 2
            ups = [functools.partial(up, c) for c in range(FF // UC)]
            outs = [functools.partial(outp, slot, c) for c in range(0, D, DC)]
            downs = [functools.partial(down, old, c) for c in range(0, D, DC)]
            takes = [functools.partial(take, slot, c) for c in range(0, D, DC)]
            if do_b:
                yb[old] = hh[...].astype(F32).reshape(FR, G, D).astype(BF)
            if do_a and do_b:
                interleave(ups, takes, [1.0] * len(ups))
                for th in outs:
                    th()
                interleave(downs, ln2s, [1.0] * len(downs))
            elif do_a:
                for th in takes + outs + ln2s:
                    th()
            else:
                for th in ups + downs:
                    th()

        for c in fetch(0, 0):
            c.start()
        for c in fetch(0, 0):
            c.wait()
        for c in fetch(1, 1):
            c.start()
        loads[1].wait()
        step(0, True, False)
        loads[2].wait()
        wd_load.wait()

        def body(b, _):
            slot = b % 2
            for c in fetch(b, slot):
                c.wait()

            @pl.when(b + 1 < NB)
            def _():
                pl.when(b + 1 >= NG)(lambda: arrive(b + 1).wait())
                for c in fetch(b + 1, (b + 1) % 2):
                    c.start()
            pl.when(b >= 3)(lambda: y_store(b - 3, (b + 1) % 2).wait())
            step(b, True, True)
            y_store(b - 1, (b + 1) % 2).start()
            return 0
        lax.fori_loop(1, NB, body, 0)

        y_store(NB - 3, (NB - 3) % 2).wait()
        step(NB, False, True)
        y_store(NB - 1, (NB - 1) % 2).start()
        for b in (NB - 2, NB - 1):
            y_store(b, b % 2).wait()

    vm = pltpu.VMEM
    pl.run_scoped(
        phase1,
        vm((2, NCOL, G * S, LANES), F32), vm((2, NCOL, G * S, LANES), F32), vm((2, 4, FR, G, D), BF), vm((T, D), BF),
        vm((2, H, 2 * EP, T), BF), vm((2, H, 2 * EP, KF), BF), vm((2, H, EP, T), BF),
        vm((SLOTS, KF, T), F32), vm((SLOTS, T, T), BF), vm((D, T), BF), vm((4, FR, G, D), BF))
    pl.run_scoped(
        phase2,
        vm((FF, D), BF), vm((2, FR, G, D), BF), vm((2, FR, G, D), BF), vm((2, FR, G, D), BF),
        vm((B, D), BF), vm((B, D), BF), vm((B, D), BF), vm((B, FF), BF))

    def drain(g, _):
        for k in (1, 2, 3):
            send(g, k).wait_send()
        return 0
    lax.fori_loop(0, NG, drain, 0)


def temporal(rcv, xs, gain, shift, wq, wo, wu, wd):
    _, FR, NPQ, _ = rcv.shape
    NG = NPQ // G
    any_spec = pl.BlockSpec(memory_space=pl.ANY)
    full = pl.BlockSpec(memory_space=pltpu.VMEM)
    vm = pltpu.VMEM
    part = jax.ShapeDtypeStruct((4, FR, NPQ, D), BF)
    toks = 4 * FR * NPQ
    flops = 2 * toks * (4 * D * D + 2 * D * FF) + 4 * toks * 4 * FR * D
    y, _, _ = pl.pallas_call(
        functools.partial(temporal_kernel, FR, NPQ),
        in_specs=[any_spec, any_spec, full, full, any_spec, any_spec, any_spec, any_spec],
        out_specs=[any_spec, any_spec, any_spec],
        out_shape=[jax.ShapeDtypeStruct((FR, 4 * NPQ, D), BF), part, part],
        scratch_shapes=[
            vm((3 * D, D), BF), vm((D, D), BF), vm((D, FF), BF),
            pltpu.SemaphoreType.DMA((4,)), pltpu.SemaphoreType.DMA((2,)), pltpu.SemaphoreType.DMA((2,)),
            pltpu.SemaphoreType.DMA((3, NG)), pltpu.SemaphoreType.DMA((3, NG)),
            pltpu.SemaphoreType.DMA((2, 2)), pltpu.SemaphoreType.DMA((2,)),
        ],
        compiler_params=pltpu.CompilerParams(
            collective_id=1, has_side_effects=True, vmem_limit_bytes=62 * 1024 * 1024),
        cost_estimate=pl.CostEstimate(flops=flops, bytes_accessed=6 * rcv.size * 2, transcendentals=0),
        name="temporal",
    )(rcv, xs, gain, shift, wq, wo, wu, wd)
    return y


def solution(mesh):
    tok_spec = P(("pod", "dp"), "sp", None, None)

    def local_step(x, gain, shift, w_qkv, w_out, w_up, w_down):
        wq = jnp.transpose(w_qkv, (0, 1, 3, 4, 2)).reshape(2, 3 * D, D)
        wo = w_out.reshape(2, D, D)
        xs, rcv = spatial(x[0], gain, shift, wq, wo, w_up, w_down)
        return temporal(rcv, xs, gain, shift, wq, wo, w_up, w_down)[None]

    return jax.shard_map(local_step, mesh=mesh, in_specs=(tok_spec, P(), P(), P(), P(), P(), P()), out_specs=tok_spec, check_vma=False)
```

time: 1590 us -> 893 us (0.56)
  Pallas kernels: 0 us -> 875 us
  matrix products: 850 us -> 0 us
  blocking collectives: 418 us -> 0 us
  other arithmetic: 262 us -> 0 us
  local copies, waits for them, and re-layouts: 52.6 us -> 16.8 us
    pallas_call x0 -> x2, Pallas kernels: none -> 875 us  [the longest x1 500 us: temporal(): pl.pallas_call(functools.partial(temporal_kernel, FR, NPQ), in_specs=[any...]
    dot_general x10 -> x0, matrix products: 850 us -> none  [the longest x2 241 us: block_tail(): jnp.dot(normed_mlp, w_up, preferred_element_type=jnp.float32)]
    all_to_all x2 -> x0, blocking collectives: 418 us -> none  [the longest x1 210 us: local_step(): by_patch = lax.all_to_all(spatial_out, 'sp', 2, 1, tiled=True)]
    sub x2 -> x0, other arithmetic: 197 us -> none  [attn_core(): attn_probs = jax.nn.softmax(scores, axis=-1).astype(jnp.bfloat16)]
    reduce_sum x6 -> x0, other arithmetic: 53.7 us -> none  [the longest x4 31.7 us: layer_norm(): var_val = jnp.mean(centered * centered, axis=-1, keepdims=True)]
    convert_element_type x3 -> x0, local copies, waits for them, and re-layouts: 45.6 us -> none  [the longest x2 32.7 us: block_tail(): (hidden.astype(jnp.float32) + down_proj.astype(jnp.float32)).astype(jnp.b...]
    unnamed x24 -> x1, local copies, waits for them, and re-layouts: 0.05 us -> 16.8 us
where the time goes in v1:
time: 893 us; the launch traced here: 892 us
  Pallas kernels  875 us (98%)
  local copies, waits for them, and re-layouts  16.8 us (2%)
    pallas_call x1, Pallas kernels, temporal(): pl.pallas_call(functools.partial(temporal_kernel, FR, NPQ), in_specs=[any...  500 us
    pallas_call x1, Pallas kernels, spatial(): pl.pallas_call(functools.partial(spatial_kernel, FR, NPQ), grid=(FR + 1,)...  375 us

profile of v1, /device:TPU:0, one launch (start us, length us, event | category | flops | bytes accessed | tf_op | source)
XLA Modules:
  0.0 892.3 jit_solution(14632168601256366986)
XLA Ops:
  0.0 375.1 %spatial.1 = (bf16[4,32,64,1152]{3,2,1,0:T(8,128)(2,1)}, bf16[4,32,64,1152]{3,2,1,0:T(8,128)(2,1)}) custom-call(bf16[32,256,1152]{2,1,0:T(8,128)(2,1)} %bitcast.7, bf16[32,256,1152]{2,1,0:T(8,128)(2,1)} %bitcast.8, bf16[2,2,1152]{2,1,0:T(2,128)(2,1)} %gain_ref.3, bf16[2,2,1152]{2,1,0:T(2,128)(2,1)} %shift_ref.3, bf16[2,3456,1152]{2,1,0:T(8,128)(2,1)} %bitcast.9, ...), custom_call_target="tpu_custom_call" | custom-call | flops 270582939648 | bytes 75497472 | tf_op jit(solution)/shard_map/spatial/pallas_call | solution.py:251
  375.1 500.1 %temporal.1 = (bf16[32,256,1152]{2,1,0:T(8,128)(2,1)}, bf16[4,32,64,1152]{3,2,1,0:T(8,128)(2,1)}, bf16[4,32,64,1152]{3,2,1,0:T(8,128)(2,1)}) custom-call(bf16[4,32,64,1152]{3,2,1,0:T(8,128)(2,1)} %get-tuple-element.8.rcv_hbm, bf16[4,32,64,1152]{3,2,1,0:T(8,128)(2,1)} %get-tuple-element.9.xs_hbm, bf16[2,2,1152]{2,1,0:T(2,128)(2,1)} %gain_ref.3, ...), custom_call_target="tpu_custom_call" | custom-call | flops 265751101440 | bytes 113246208 | tf_op jit(solution)/shard_map/temporal/pallas_call | solution.py:594
  875.2 16.8 %copy.9 = bf16[1,32,256,1152]{3,2,1,0:T(8,128)(2,1)} copy(bf16[1,32,256,1152]{3,2,1,0:T(8,128)(2,1)} %bitcast.6) | data formatting | bytes 37748736
